TPU v7x, 32 devices: a whole 2x2x4 slice. The times are simulated.
32 devices in a mesh: dom: 32 (over z, y, x, core).
Axes of the slice: x: 2, y: 2, z: 4, core: 2. Of those that a mesh axis runs over, the one named last changes fastest.
Arguments:
- node_emb: bfloat16 [16384, 64], P('dom'), may hold values from -6 to 6
- hub_emb: bfloat16 [256, 64], replicated, may hold values from -6 to 6
- tile_vals: bfloat16 [4096, 128, 128], P('dom')
- tile_col: int32 [4096], P('dom'), may hold values from 0 to 5
- tile_dest: int32 [4096], P('dom'), may hold values from 0 to 29, as said below
Outputs:
- node_out: float32 [16384, 64], P('dom')
- hub_out: float32 [256, 64], replicated
Inputs may be any that keep to these rules, and one draw needn't show every extreme that they name: tile_dest below 28 names a partition offset from -3 to 3 and a block of that partition; from 28 up it names a hub block. tile_col below 4 names one of the holding partition's own blocks; from 4 up it names a hub block.
All inputs are finite; a program needn't handle non-finite values.
Results may differ from a plain program's by a relative error of at most 0.0003.
Values sent between devices are 32-bit elements.
A program may use at most 64 MiB of HBM per device.

v0:
```python
import jax
import jax.numpy as jnp
from jax import lax
from jax.sharding import PartitionSpec as P

REACH_BITS = 2
LAYERS = 2


def shifted(block, axis, distance):
    devices = range(lax.axis_size(axis))
    route = [((i - distance) % len(devices), i) for i in devices]
    return lax.ppermute(block, axis, route)


def route_partials(spread, farthest):
    overall = spread[farthest]
    for heading in (1, -1):
        for distance in range(1, farthest + 1):
            overall = overall + shifted(
                spread[farthest + heading * distance], "dom", heading * distance
            )
    return overall


def shards(node_emb, hub_emb, tile_vals, tile_col, tile_dest):
    tile_size = tile_vals.shape[1]
    features = node_emb.shape[1]
    dev_rows = node_emb.shape[0]
    own_blocks = dev_rows // tile_size
    hub_rows = hub_emb.shape[0]
    hub_blocks = hub_rows // tile_size
    tile_count = tile_vals.shape[0]
    farthest = 2**REACH_BITS - 1
    slot_count = 2 * farthest + 1
    target_count = slot_count * own_blocks + hub_blocks
    one_hot = (tile_dest[None, :] == jnp.arange(target_count, dtype=jnp.int32)[:, None]).astype(
        jnp.float32
    )
    current_node = node_emb
    current_hub = hub_emb
    node_total = node_emb.astype(jnp.float32)
    hub_total = hub_emb.astype(jnp.float32)
    for layer_index in range(LAYERS):
        sources = jnp.concatenate([current_node, current_hub], 0).reshape(
            own_blocks + hub_blocks, tile_size, features
        )
        picked = jnp.take(sources, tile_col, axis=0)
        products = jnp.einsum("tij,tjd->tid", tile_vals, picked, preferred_element_type=jnp.float32)
        summed = jnp.dot(
            one_hot,
            products.reshape(tile_count, tile_size * features),
            precision=lax.Precision.HIGHEST,
            preferred_element_type=jnp.float32,
        )
        spread = summed[: slot_count * own_blocks].reshape(slot_count, dev_rows, features)
        hub_part = summed[slot_count * own_blocks :].reshape(hub_rows, features)
        hub_sum = lax.psum(hub_part, "dom")
        node_sum = route_partials(spread, farthest)
        node_total = node_total + node_sum
        hub_total = hub_total + hub_sum
        current_node = node_sum.astype(jnp.bfloat16)
        current_hub = hub_sum.astype(jnp.bfloat16)
    return (node_total / float(LAYERS + 1), hub_total / float(LAYERS + 1))


def solution(mesh):
    in_specs = (P("dom", None), P(), P("dom", None, None), P("dom"), P("dom"))
    out_specs = (P("dom", None), P())
    return jax.shard_map(shards, mesh=mesh, in_specs=in_specs, out_specs=out_specs, check_vma=False)
```

profile of v0, /device:TPU:0, one launch (start us, length us, event | category | flops | bytes accessed | tf_op | source)
XLA Modules:
  0.0 331.4 jit_solution(637796549837110401)
XLA Ops:
  7.2 0.7 compare_select_fusion
  7.9 0.7 compare_and_fusion
  8.5 0.9 copy_bitcast_fusion
  9.4 1.0 gather_fusion
  10.4 7.1 %convolution_bitcast_fusion.1 = f32[128,128,64]{1,2,0:T(8,128)} fusion(bf16[128,128,128]{2,1,0:T(8,128)(2,1)} %param.9, bf16[128,128,64]{1,2,0:T(8,128)(2,1)S(1)} %gather_fusion, pred[128]{0:T(512)(128)(4,1)S(1)} %compare_and_fusion), kind=kOutput, calls=%fused_computation.3 | convolution fusion | flops 269484032 | bytes 10485888 | tf_op jit(solution)/shard_map/tij,tjd->tid/dot_general | solution.py:49
  17.5 5.5 %copy.25 = f32[128,128,64]{0,2,1:T(8,128)} copy(f32[128,128,64]{1,2,0:T(8,128)} %convolution_bitcast_fusion.1) | data formatting | bytes 8388608 | tf_op jit(solution)/shard_map/tij,tjd->tid/dot_general | solution.py:49
  22.9 4.6 %fusion.7 = f32[30,8192]{1,0:T(8,128)S(1)} fusion(f32[128,8192]{0,1:T(8,128)} %bitcast.16, s32[128]{0:T(128)S(1)} %copy-done.3), kind=kOutput, calls=%fused_computation.18 | convolution fusion | flops 377491200 | bytes 5177856 | tf_op jit(solution)/shard_map/dot_general | solution.py:50
  27.5 0.1 fusion.14
  27.7 0.2 squeeze.43
  27.8 0.5 collective-permute-start
  28.4 0.2 squeeze.44
  28.5 2.5 collective-permute-start.1
  31.1 0.2 squeeze.45
  31.3 2.4 collective-permute-start.2
  33.7 0.9 squeeze.46
  34.6 3.0 collective-permute-start.3
  37.5 0.9 squeeze.47
  38.4 1.2 collective-permute-start.4
  39.6 0.9 squeeze.48
  40.5 2.4 collective-permute-done
  42.9 0.8 reshape.60
  43.7 0.2 all-reduce.5.cloned.1.call-start
  43.9 0.2 squeeze.42
  44.1 124.6 %all-reduce.3.cloned.1.call-done = f32[256,64]{1,0:T(8,128)} async-done(((f32[256,64]{1,0:T(8,128)}), f32[256,64]{1,0:T(8,128)}) %all-reduce.3.cloned.1.call-update) | async-done | bytes 65552 | tf_op jit(solution)/shard_map/psum | solution.py:58
  168.7 0.9 convert_element_type.15
  169.8 0.1 copy.27
  169.9 1.0 gather_fusion.1
  170.9 7.1 %convolution_bitcast_fusion = f32[128,128,64]{1,2,0:T(8,128)} fusion(bf16[128,128,128]{2,1,0:T(8,128)(2,1)} %param.9, bf16[128,128,64]{1,2,0:T(8,128)(2,1)S(1)} %gather_fusion.1, pred[128]{0:T(512)(128)(4,1)S(1)} %compare_and_fusion), kind=kOutput, calls=%fused_computation.2 | convolution fusion | flops 269484032 | bytes 10485888 | tf_op jit(solution)/shard_map/tij,tjd->tid/dot_general | solution.py:49
  178.0 5.4 %copy.28 = f32[128,128,64]{0,2,1:T(8,128)} copy(f32[128,128,64]{1,2,0:T(8,128)} %convolution_bitcast_fusion) | data formatting | bytes 8388608 | tf_op jit(solution)/shard_map/tij,tjd->tid/dot_general | solution.py:49
  183.4 4.6 %fusion.6 = f32[30,8192]{1,0:T(8,128)S(1)} fusion(f32[128,8192]{0,1:T(8,128)} %bitcast.17, s32[128]{0:T(128)S(1)} %copy-done.3), kind=kOutput, calls=%fused_computation.17 | convolution fusion | flops 377491200 | bytes 5177856 | tf_op jit(solution)/shard_map/dot_general | solution.py:50
  188.1 0.1 fusion.13
  188.2 0.2 squeeze.54
  188.4 3.3 collective-permute-start.10
  191.7 0.8 reshape.63
  192.8 0.2 squeeze.55
  193.0 0.9 squeeze.50
  193.9 1.6 collective-permute-start.6
  195.5 0.9 squeeze.51
  196.4 0.6 collective-permute-start.7
  196.9 0.9 squeeze.52
  197.8 0.9 squeeze.53
  198.7 0.2 squeeze.49
  198.9 0.8 collective-permute-done.10
  199.7 3.6 %collective-permute-start.9 = (f32[512,64]{1,0:T(8,128)}, f32[512,64]{1,0:T(8,128)S(1)}, u32[]{:S(2)}, u32[]{:S(2)}) collective-permute-start(f32[512,64]{1,0:T(8,128)} %squeeze.53), channel_id=1, source_target_pairs={{1,0},{2,1},{3,2},{4,3},{5,4},{6,5},{7,6},{8,7},{9,8},{10,9},{11,1... | collective-permute-start | bytes 393224 | tf_op jit(solution)/shard_map/ppermute | solution.py:13
  203.3 118.6 %all-reduce.5.cloned.1.call-done = f32[256,64]{1,0:T(8,128)} async-done(((f32[256,64]{1,0:T(8,128)}), f32[256,64]{1,0:T(8,128)}) %all-reduce.5.cloned.1.call-update) | async-done | bytes 65552 | tf_op jit(solution)/shard_map/psum | solution.py:58
  321.9 0.9 add_multiply_fusion.1
  322.9 0.7 copy.31
  323.7 0.8 copy.30
  (32 shorter events, 0.7 us)
Async XLA Ops:
  7.2 161.5 %all-reduce.3.cloned.1.call-start = ((), (), s32[]{:S(2)}) async-start(), calls=%async_computation | async-start | bytes 262144 | tf_op jit(solution)/shard_map/psum | solution.py:58
  17.5 5.5 %copy-start.3 = (s32[128]{0:T(128)S(1)}, s32[128]{0:T(128)}, u32[]{:S(2)}) copy-start(s32[128]{0:T(128)} %param.11) | copy-start | bytes 1540
  27.8 15.0 %collective-permute-start = (f32[512,64]{1,0:T(8,128)S(1)}, f32[512,64]{1,0:T(8,128)S(1)}, u32[]{:S(2)}, u32[]{:S(2)}) collective-permute-start(f32[512,64]{1,0:T(8,128)S(1)} %squeeze.43), channel_id=1, source_target_pairs={{31,0},{0,1},{1,2},{2,3},{3,4},{4,5},{5,6},{6,7},{7,8},{8,9},{9,10... | collective-permute-start | bytes 393224 | tf_op jit(solution)/shard_map/ppermute | solution.py:13
  28.5 141.1 %collective-permute-start.1 = (f32[512,64]{1,0:T(8,128)S(1)}, f32[512,64]{1,0:T(8,128)S(1)}, u32[]{:S(2)}, u32[]{:S(2)}) collective-permute-start(f32[512,64]{1,0:T(8,128)S(1)} %squeeze.44), channel_id=1, source_target_pairs={{30,0},{31,1},{0,2},{1,3},{2,4},{3,5},{4,6},{5,7},{6,8},{7,9},{8,1... | collective-permute-start | bytes 393224 | tf_op jit(solution)/shard_map/ppermute | solution.py:13
  31.3 138.4 %collective-permute-start.2 = (f32[512,64]{1,0:T(8,128)S(1)}, f32[512,64]{1,0:T(8,128)S(1)}, u32[]{:S(2)}, u32[]{:S(2)}) collective-permute-start(f32[512,64]{1,0:T(8,128)S(1)} %squeeze.45), channel_id=1, source_target_pairs={{29,0},{30,1},{31,2},{0,3},{1,4},{2,5},{3,6},{4,7},{5,8},{6,9},{7,... | collective-permute-start | bytes 393224 | tf_op jit(solution)/shard_map/ppermute | solution.py:13
  34.6 135.0 %collective-permute-start.3 = (f32[512,64]{1,0:T(8,128)}, f32[512,64]{1,0:T(8,128)S(1)}, u32[]{:S(2)}, u32[]{:S(2)}) collective-permute-start(f32[512,64]{1,0:T(8,128)} %squeeze.46), channel_id=1, source_target_pairs={{1,0},{2,1},{3,2},{4,3},{5,4},{6,5},{7,6},{8,7},{9,8},{10,9},{11,1... | collective-permute-start | bytes 393224 | tf_op jit(solution)/shard_map/ppermute | solution.py:13
  38.4 131.2 %collective-permute-start.4 = (f32[512,64]{1,0:T(8,128)}, f32[512,64]{1,0:T(8,128)S(1)}, u32[]{:S(2)}, u32[]{:S(2)}) collective-permute-start(f32[512,64]{1,0:T(8,128)} %squeeze.47), channel_id=1, source_target_pairs={{2,0},{3,1},{4,2},{5,3},{6,4},{7,5},{8,6},{9,7},{10,8},{11,9},{12,... | collective-permute-start | bytes 393224 | tf_op jit(solution)/shard_map/ppermute | solution.py:13
  42.9 126.8 %collective-permute-start.5 = (f32[512,64]{1,0:T(8,128)}, f32[512,64]{1,0:T(8,128)S(1)}, u32[]{:S(2)}, u32[]{:S(2)}) collective-permute-start(f32[512,64]{1,0:T(8,128)} %squeeze.48), channel_id=1, source_target_pairs={{3,0},{4,1},{5,2},{6,3},{7,4},{8,5},{9,6},{10,7},{11,8},{12,9},{13... | collective-permute-start | bytes 393224 | tf_op jit(solution)/shard_map/ppermute | solution.py:13
  43.7 278.2 %all-reduce.5.cloned.1.call-start = ((), (), s32[]{:S(2)}) async-start(), calls=%async_computation.1 | async-start | bytes 262144 | tf_op jit(solution)/shard_map/psum | solution.py:58
  183.4 9.1 %copy-start.1 = (bf16[512,64]{0,1:T(8,128)(2,1)S(1)}, bf16[512,64]{0,1:T(8,128)(2,1)}, u32[]{:S(2)}) copy-start(bf16[512,64]{0,1:T(8,128)(2,1)} %param.7) | copy-start | bytes 196612
  183.4 9.2 %copy-start.2 = (bf16[256,64]{0,1:T(8,128)(2,1)S(1)}, bf16[256,64]{0,1:T(8,128)(2,1)}, u32[]{:S(2)}) copy-start(bf16[256,64]{0,1:T(8,128)(2,1)} %param.8) | copy-start | bytes 98308
  183.4 138.5 %copy-start = (f32[256,64]{1,0:T(8,128)S(1)}, f32[256,64]{1,0:T(8,128)}, u32[]{:S(2)}) copy-start(f32[256,64]{1,0:T(8,128)} %all-reduce.3.cloned.1.call-done) | copy-start | bytes 196612
  188.4 11.3 %collective-permute-start.10 = (f32[512,64]{1,0:T(8,128)S(1)}, f32[512,64]{1,0:T(8,128)S(1)}, u32[]{:S(2)}, u32[]{:S(2)}) collective-permute-start(f32[512,64]{1,0:T(8,128)S(1)} %squeeze.54), channel_id=1, source_target_pairs={{2,0},{3,1},{4,2},{5,3},{6,4},{7,5},{8,6},{9,7},{10,8},{11,9},{12,... | collective-permute-start | bytes 393224 | tf_op jit(solution)/shard_map/ppermute | solution.py:13
  193.0 130.6 %collective-permute-start.11 = (f32[512,64]{1,0:T(8,128)S(1)}, f32[512,64]{1,0:T(8,128)S(1)}, u32[]{:S(2)}, u32[]{:S(2)}) collective-permute-start(f32[512,64]{1,0:T(8,128)S(1)} %squeeze.55), channel_id=1, source_target_pairs={{3,0},{4,1},{5,2},{6,3},{7,4},{8,5},{9,6},{10,7},{11,8},{12,9},{13... | collective-permute-start | bytes 393224 | tf_op jit(solution)/shard_map/ppermute | solution.py:13
  193.9 129.7 %collective-permute-start.6 = (f32[512,64]{1,0:T(8,128)}, f32[512,64]{1,0:T(8,128)S(1)}, u32[]{:S(2)}, u32[]{:S(2)}) collective-permute-start(f32[512,64]{1,0:T(8,128)} %squeeze.50), channel_id=1, source_target_pairs={{31,0},{0,1},{1,2},{2,3},{3,4},{4,5},{5,6},{6,7},{7,8},{8,9},{9,10... | collective-permute-start | bytes 393224 | tf_op jit(solution)/shard_map/ppermute | solution.py:13
  196.4 127.2 %collective-permute-start.7 = (f32[512,64]{1,0:T(8,128)}, f32[512,64]{1,0:T(8,128)S(1)}, u32[]{:S(2)}, u32[]{:S(2)}) collective-permute-start(f32[512,64]{1,0:T(8,128)} %squeeze.51), channel_id=1, source_target_pairs={{30,0},{31,1},{0,2},{1,3},{2,4},{3,5},{4,6},{5,7},{6,8},{7,9},{8,1... | collective-permute-start | bytes 393224 | tf_op jit(solution)/shard_map/ppermute | solution.py:13
  197.8 125.8 %collective-permute-start.8 = (f32[512,64]{1,0:T(8,128)}, f32[512,64]{1,0:T(8,128)S(1)}, u32[]{:S(2)}, u32[]{:S(2)}) collective-permute-start(f32[512,64]{1,0:T(8,128)} %squeeze.52), channel_id=1, source_target_pairs={{29,0},{30,1},{31,2},{0,3},{1,4},{2,5},{3,6},{4,7},{5,8},{6,9},{7,... | collective-permute-start | bytes 393224 | tf_op jit(solution)/shard_map/ppermute | solution.py:13
  199.7 123.9 %collective-permute-start.9 = (f32[512,64]{1,0:T(8,128)}, f32[512,64]{1,0:T(8,128)S(1)}, u32[]{:S(2)}, u32[]{:S(2)}) collective-permute-start(f32[512,64]{1,0:T(8,128)} %squeeze.53), channel_id=1, source_target_pairs={{1,0},{2,1},{3,2},{4,3},{5,4},{6,5},{7,6},{8,7},{9,8},{10,9},{11,1... | collective-permute-start | bytes 393224 | tf_op jit(solution)/shard_map/ppermute | solution.py:13
Sparse Core Ops, SparseCore 0:
  43.8 124.8 all-reduce.2
  192.7 129.2 all-reduce.4
where the time goes:
time: 332 us; the launch traced here: 331 us
  waiting for transfers between devices  246 us (74%)
  local copies, waits for them, and re-layouts  24.1 us (7%)
  matrix products  23.3 us (7%)
  starting transfers between devices  19 us (6%)
  between operations  14.2 us (4%)
  other arithmetic  4.29 us (1%)
    psum x2, waiting for transfers between devices, shards(): hub_sum = lax.psum(hub_part, 'dom')  243 us
    ppermute x12, starting transfers between devices, shifted(): return lax.ppermute(block, axis, route)  18.7 us
    dot_general x2, matrix products, shards(): jnp.einsum('tij,tjd->tid', tile_vals, picked, preferred_element_type=jnp....  14.1 us
    dot_general x2, local copies, waits for them, and re-layouts, shards(): jnp.einsum('tij,tjd->tid', tile_vals, picked, preferred_element_type=jnp....  10.9 us
    dot_general x2, matrix products, shards(): jnp.dot(one_hot, products.reshape(tile_count, tile_size * features), prec...  9.19 us
    squeeze x12, local copies, waits for them, and re-layouts, route_partials(): spread[farthest + heading * distance]  7.08 us
  transfers between devices with their start and end apart: 14, of which 4 were waited for; matrix products, arithmetic and copies ran while one was open for 3% of the time, Pallas kernels for 0%

commit v1 on v0

--- a/solution.py
+++ b/solution.py
@@ -55,7 +55,11 @@
         )
         spread = summed[: slot_count * own_blocks].reshape(slot_count, dev_rows, features)
         hub_part = summed[slot_count * own_blocks :].reshape(hub_rows, features)
-        hub_sum = lax.psum(hub_part, "dom")
+        hub_sum = hub_part
+        for hop in (1, 2, 4, 8, 16):
+            hub_sum = hub_sum + lax.ppermute(
+                hub_sum, "dom", [(dev, dev ^ hop) for dev in range(32)]
+            )
         node_sum = route_partials(spread, farthest)
         node_total = node_total + node_sum
         hub_total = hub_total + hub_sum

time: 332 us -> 137 us (0.41)
  waiting for transfers between devices: 246 us -> 65.6 us
  between operations: 14.2 us -> 0.87 us
    psum x2 -> x0, waiting for transfers between devices: 243 us -> none  [shards(): hub_sum = lax.psum(hub_part, 'dom')]
    ppermute x0 -> x10, waiting for transfers between devices: none -> 33.5 us  [shards(): lax.ppermute(hub_sum, 'dom', [(dev, dev ^ hop) for dev in range(32)])]
    ppermute x12, waiting for transfers between devices: 3.24 us -> 32 us  [shifted(): return lax.ppermute(block, axis, route)]
    ppermute x0 -> x10, starting transfers between devices: none -> 6.18 us  [shards(): lax.ppermute(hub_sum, 'dom', [(dev, dev ^ hop) for dev in range(32)])]
    ppermute x12, starting transfers between devices: 18.7 us -> 14.5 us  [shifted(): return lax.ppermute(block, axis, route)]
  transfers between devices with their start and end apart: 14 -> 22, of which waited for: 4 -> 14; matrix products, arithmetic and copies ran while one was open for 3% -> 7% of each run, Pallas kernels for 0% -> 0%
where the time goes in v1:
time: 137 us
  waiting for transfers between devices  65.6 us (48%)
  matrix products  23.3 us (17%)
  local copies, waits for them, and re-layouts  23 us (17%)
  starting transfers between devices  20.7 us (15%)
  other arithmetic  3.52 us (3%)
    ppermute x10, waiting for transfers between devices, shards(): lax.ppermute(hub_sum, 'dom', [(dev, dev ^ hop) for dev in range(32)])  33.5 us
    ppermute x12, waiting for transfers between devices, shifted(): return lax.ppermute(block, axis, route)  32 us
    ppermute x12, starting transfers between devices, shifted(): return lax.ppermute(block, axis, route)  14.5 us
    dot_general x2, matrix products, shards(): jnp.einsum('tij,tjd->tid', tile_vals, picked, preferred_element_type=jnp....  14.1 us
    dot_general x2, local copies, waits for them, and re-layouts, shards(): jnp.einsum('tij,tjd->tid', tile_vals, picked, preferred_element_type=jnp....  11 us
    dot_general x2, matrix products, shards(): jnp.dot(one_hot, products.reshape(tile_count, tile_size * features), prec...  9.16 us
    squeeze x12, local copies, waits for them, and re-layouts, route_partials(): spread[farthest + heading * distance]  7.18 us
    ppermute x10, starting transfers between devices, shards(): lax.ppermute(hub_sum, 'dom', [(dev, dev ^ hop) for dev in range(32)])  6.18 us
  transfers between devices with their start and end apart: 22, of which 14 were waited for; matrix products, arithmetic and copies ran while one was open for 7% of the time, Pallas kernels for 0%

profile of v1, /device:TPU:0, one launch (start us, length us, event | category | flops | bytes accessed | tf_op | source)
XLA Modules:
  0.0 136.9 jit_solution(3921920130993210558)
XLA Ops:
  0.6 0.7 compare_select_fusion
  1.3 0.7 compare_and_fusion
  2.0 0.9 copy_bitcast_fusion
  2.8 1.0 gather_fusion
  3.8 7.1 %convolution_bitcast_fusion.1 = f32[128,128,64]{1,2,0:T(8,128)} fusion(bf16[128,128,128]{2,1,0:T(8,128)(2,1)} %param.9, bf16[128,128,64]{1,2,0:T(8,128)(2,1)S(1)} %gather_fusion, pred[128]{0:T(512)(128)(4,1)S(1)} %compare_and_fusion), kind=kOutput, calls=%fused_computation.3 | convolution fusion | flops 269484032 | bytes 10485888 | tf_op jit(solution)/shard_map/tij,tjd->tid/dot_general | solution.py:49
  10.9 5.5 %copy.27 = f32[128,128,64]{0,2,1:T(8,128)} copy(f32[128,128,64]{1,2,0:T(8,128)} %convolution_bitcast_fusion.1) | data formatting | bytes 8388608 | tf_op jit(solution)/shard_map/tij,tjd->tid/dot_general | solution.py:49
  16.4 4.6 %fusion.7 = f32[30,8192]{1,0:T(8,128)S(1)} fusion(f32[128,8192]{0,1:T(8,128)} %bitcast.16, s32[128]{0:T(128)S(1)} %copy-done.3), kind=kOutput, calls=%fused_computation.19 | convolution fusion | flops 377491200 | bytes 5177856 | tf_op jit(solution)/shard_map/dot_general | solution.py:50
  21.1 0.5 collective-permute-start.6
  21.7 1.0 collective-permute-done.6
  22.7 2.9 %collective-permute-start.7 = (f32[256,64]{1,0:T(8,128)S(1)}, f32[256,64]{1,0:T(8,128)S(1)}, u32[]{:S(2)}, u32[]{:S(2)}) collective-permute-start(f32[256,64]{1,0:T(8,128)S(1)} %add.91), channel_id=1, source_target_pairs={{0,2},{1,3},{2,0},{3,1},{4,6},{5,7},{6,4},{7,5},{8,10},{9,11},{10,... | collective-permute-start | bytes 196616 | tf_op jit(solution)/shard_map/ppermute | solution.py:60
  25.7 0.2 squeeze.43
  26.0 3.5 %collective-permute-done.7 = f32[256,64]{1,0:T(8,128)S(1)} collective-permute-done((f32[256,64]{1,0:T(8,128)S(1)}, f32[256,64]{1,0:T(8,128)S(1)}, u32[]{:S(2)}, u32[]{:S(2)}) %collective-permute-start.7) | collective-permute-done | bytes 65568 | tf_op jit(solution)/shard_map/ppermute | solution.py:60
  29.5 1.8 %collective-permute-start.8 = (f32[256,64]{1,0:T(8,128)S(1)}, f32[256,64]{1,0:T(8,128)S(1)}, u32[]{:S(2)}, u32[]{:S(2)}) collective-permute-start(f32[256,64]{1,0:T(8,128)S(1)} %add.92), channel_id=1, source_target_pairs={{0,4},{1,5},{2,6},{3,7},{4,0},{5,1},{6,2},{7,3},{8,12},{9,13},{10,... | collective-permute-start | bytes 196616 | tf_op jit(solution)/shard_map/ppermute | solution.py:60
  31.3 6.0 %collective-permute-done.8 = f32[256,64]{1,0:T(8,128)S(1)} collective-permute-done((f32[256,64]{1,0:T(8,128)S(1)}, f32[256,64]{1,0:T(8,128)S(1)}, u32[]{:S(2)}, u32[]{:S(2)}) %collective-permute-start.8) | collective-permute-done | bytes 65568 | tf_op jit(solution)/shard_map/ppermute | solution.py:60
  37.3 0.7 collective-permute-start.9
  38.2 0.7 collective-permute-start.1
  39.1 0.9 squeeze.46
  40.0 5.3 %collective-permute-start.3 = (f32[512,64]{1,0:T(8,128)}, f32[512,64]{1,0:T(8,128)S(1)}, u32[]{:S(2)}, u32[]{:S(2)}) collective-permute-start(f32[512,64]{1,0:T(8,128)} %squeeze.46), channel_id=1, source_target_pairs={{1,0},{2,1},{3,2},{4,3},{5,4},{6,5},{7,6},{8,7},{9,8},{10,9},{11,1... | collective-permute-start | bytes 393224 | tf_op jit(solution)/shard_map/ppermute | solution.py:13
  45.3 0.9 squeeze.47
  46.2 0.9 squeeze.48
  47.1 0.6 collective-permute-start.4
  47.7 0.5 collective-permute-start.5
  48.4 5.1 %collective-permute-done.1 = f32[512,64]{1,0:T(8,128)S(1)} collective-permute-done((f32[512,64]{1,0:T(8,128)S(1)}, f32[512,64]{1,0:T(8,128)S(1)}, u32[]{:S(2)}, u32[]{:S(2)}) %collective-permute-start.1) | collective-permute-done | bytes 131104 | tf_op jit(solution)/shard_map/ppermute | solution.py:13
  53.5 6.3 %collective-permute-done.4 = f32[512,64]{1,0:T(8,128)S(1)} collective-permute-done((f32[512,64]{1,0:T(8,128)}, f32[512,64]{1,0:T(8,128)S(1)}, u32[]{:S(2)}, u32[]{:S(2)}) %collective-permute-start.4) | collective-permute-done | bytes 131104 | tf_op jit(solution)/shard_map/ppermute | solution.py:13
  59.8 5.0 %collective-permute-done.5 = f32[512,64]{1,0:T(8,128)S(1)} collective-permute-done((f32[512,64]{1,0:T(8,128)}, f32[512,64]{1,0:T(8,128)S(1)}, u32[]{:S(2)}, u32[]{:S(2)}) %collective-permute-start.5) | collective-permute-done | bytes 131104 | tf_op jit(solution)/shard_map/ppermute | solution.py:13
  64.8 5.4 %collective-permute-done.10 = f32[256,64]{1,0:T(8,128)S(1)} collective-permute-done((f32[256,64]{1,0:T(8,128)S(1)}, f32[256,64]{1,0:T(8,128)S(1)}, u32[]{:S(2)}, u32[]{:S(2)}) %collective-permute-start.10) | collective-permute-done | bytes 65568 | tf_op jit(solution)/shard_map/ppermute | solution.py:60
  70.4 1.0 gather_fusion.1
  71.4 7.1 %convolution_bitcast_fusion = f32[128,128,64]{1,2,0:T(8,128)} fusion(bf16[128,128,128]{2,1,0:T(8,128)(2,1)} %param.9, bf16[128,128,64]{1,2,0:T(8,128)(2,1)S(1)} %gather_fusion.1, pred[128]{0:T(512)(128)(4,1)S(1)} %compare_and_fusion), kind=kOutput, calls=%fused_computation.2 | convolution fusion | flops 269484032 | bytes 10485888 | tf_op jit(solution)/shard_map/tij,tjd->tid/dot_general | solution.py:49
  78.4 5.5 %copy.30 = f32[128,128,64]{0,2,1:T(8,128)} copy(f32[128,128,64]{1,2,0:T(8,128)} %convolution_bitcast_fusion) | data formatting | bytes 8388608 | tf_op jit(solution)/shard_map/tij,tjd->tid/dot_general | solution.py:49
  84.0 4.6 %fusion.6 = f32[30,8192]{1,0:T(8,128)S(1)} fusion(f32[128,8192]{0,1:T(8,128)} %bitcast.17, s32[128]{0:T(128)S(1)} %copy-done.3), kind=kOutput, calls=%fused_computation.18 | convolution fusion | flops 377491200 | bytes 5177856 | tf_op jit(solution)/shard_map/dot_general | solution.py:50
  88.8 1.3 collective-permute-done.17
  90.4 0.2 squeeze.50
  90.7 5.8 %collective-permute-done.18 = f32[256,64]{1,0:T(8,128)S(1)} collective-permute-done((f32[256,64]{1,0:T(8,128)S(1)}, f32[256,64]{1,0:T(8,128)S(1)}, u32[]{:S(2)}, u32[]{:S(2)}) %collective-permute-start.18) | collective-permute-done | bytes 65568 | tf_op jit(solution)/shard_map/ppermute | solution.py:60
  96.7 6.1 %collective-permute-done.19 = f32[256,64]{1,0:T(8,128)S(1)} collective-permute-done((f32[256,64]{1,0:T(8,128)S(1)}, f32[256,64]{1,0:T(8,128)S(1)}, u32[]{:S(2)}, u32[]{:S(2)}) %collective-permute-start.19) | collective-permute-done | bytes 65568 | tf_op jit(solution)/shard_map/ppermute | solution.py:60
  102.9 0.9 squeeze.51
  104.0 0.8 collective-permute-start.13
  104.7 0.9 squeeze.53
  105.6 5.8 %collective-permute-start.14 = (f32[512,64]{1,0:T(8,128)}, f32[512,64]{1,0:T(8,128)S(1)}, u32[]{:S(2)}, u32[]{:S(2)}) collective-permute-start(f32[512,64]{1,0:T(8,128)} %squeeze.53), channel_id=1, source_target_pairs={{1,0},{2,1},{3,2},{4,3},{5,4},{6,5},{7,6},{8,7},{9,8},{10,9},{11,1... | collective-permute-start | bytes 393224 | tf_op jit(solution)/shard_map/ppermute | solution.py:13
  111.5 0.9 squeeze.54
  112.3 0.9 squeeze.55
  113.3 0.5 collective-permute-start.16
  114.2 0.9 add.107
  115.2 4.1 %collective-permute-done.12 = f32[512,64]{1,0:T(8,128)S(1)} collective-permute-done((f32[512,64]{1,0:T(8,128)}, f32[512,64]{1,0:T(8,128)S(1)}, u32[]{:S(2)}, u32[]{:S(2)}) %collective-permute-start.12) | collective-permute-done | bytes 131104 | tf_op jit(solution)/shard_map/ppermute | solution.py:13
  119.3 6.4 %collective-permute-done.15 = f32[512,64]{1,0:T(8,128)S(1)} collective-permute-done((f32[512,64]{1,0:T(8,128)}, f32[512,64]{1,0:T(8,128)S(1)}, u32[]{:S(2)}, u32[]{:S(2)}) %collective-permute-start.15) | collective-permute-done | bytes 131104 | tf_op jit(solution)/shard_map/ppermute | solution.py:13
  125.7 5.2 %collective-permute-done.16 = f32[512,64]{1,0:T(8,128)S(1)} collective-permute-done((f32[512,64]{1,0:T(8,128)}, f32[512,64]{1,0:T(8,128)S(1)}, u32[]{:S(2)}, u32[]{:S(2)}) %collective-permute-start.16) | collective-permute-done | bytes 131104 | tf_op jit(solution)/shard_map/ppermute | solution.py:13
  131.0 0.8 copy.32
  131.8 4.3 %collective-permute-done.21 = f32[256,64]{1,0:T(8,128)S(1)} collective-permute-done((f32[256,64]{1,0:T(8,128)S(1)}, f32[256,64]{1,0:T(8,128)S(1)}, u32[]{:S(2)}, u32[]{:S(2)}) %collective-permute-start.21) | collective-permute-done | bytes 65568 | tf_op jit(solution)/shard_map/ppermute | solution.py:60
  136.2 0.7 copy.33
  (54 shorter events, 2.9 us)
Async XLA Ops:
  10.9 5.5 %copy-start.3 = (s32[128]{0:T(128)S(1)}, s32[128]{0:T(128)}, u32[]{:S(2)}) copy-start(s32[128]{0:T(128)} %param.11) | copy-start | bytes 1540
  21.1 1.5 %collective-permute-start.6 = (f32[256,64]{1,0:T(8,128)S(1)}, f32[256,64]{1,0:T(8,128)S(1)}, u32[]{:S(2)}, u32[]{:S(2)}) collective-permute-start(f32[256,64]{1,0:T(8,128)S(1)} %reshape.60), channel_id=1, source_target_pairs={{0,1},{1,0},{2,3},{3,2},{4,5},{5,4},{6,7},{7,6},{8,9},{9,8},{10,11... | collective-permute-start | bytes 196616 | tf_op jit(solution)/shard_map/ppermute | solution.py:60
  22.7 6.8 %collective-permute-start.7 = (f32[256,64]{1,0:T(8,128)S(1)}, f32[256,64]{1,0:T(8,128)S(1)}, u32[]{:S(2)}, u32[]{:S(2)}) collective-permute-start(f32[256,64]{1,0:T(8,128)S(1)} %add.91), channel_id=1, source_target_pairs={{0,2},{1,3},{2,0},{3,1},{4,6},{5,7},{6,4},{7,5},{8,10},{9,11},{10,... | collective-permute-start | bytes 196616 | tf_op jit(solution)/shard_map/ppermute | solution.py:60
  25.9 21.2 %collective-permute-start = (f32[512,64]{1,0:T(8,128)S(1)}, f32[512,64]{1,0:T(8,128)S(1)}, u32[]{:S(2)}, u32[]{:S(2)}) collective-permute-start(f32[512,64]{1,0:T(8,128)S(1)} %squeeze.43), channel_id=1, source_target_pairs={{31,0},{0,1},{1,2},{2,3},{3,4},{4,5},{5,6},{6,7},{7,8},{8,9},{9,10... | collective-permute-start | bytes 393224 | tf_op jit(solution)/shard_map/ppermute | solution.py:13
  29.5 7.8 %collective-permute-start.8 = (f32[256,64]{1,0:T(8,128)S(1)}, f32[256,64]{1,0:T(8,128)S(1)}, u32[]{:S(2)}, u32[]{:S(2)}) collective-permute-start(f32[256,64]{1,0:T(8,128)S(1)} %add.92), channel_id=1, source_target_pairs={{0,4},{1,5},{2,6},{3,7},{4,0},{5,1},{6,2},{7,3},{8,12},{9,13},{10,... | collective-permute-start | bytes 196616 | tf_op jit(solution)/shard_map/ppermute | solution.py:60
  37.3 10.4 %collective-permute-start.9 = (f32[256,64]{1,0:T(8,128)S(1)}, f32[256,64]{1,0:T(8,128)S(1)}, u32[]{:S(2)}, u32[]{:S(2)}) collective-permute-start(f32[256,64]{1,0:T(8,128)S(1)} %add.93), channel_id=1, source_target_pairs={{0,8},{1,9},{2,10},{3,11},{4,12},{5,13},{6,14},{7,15},{8,0},{9,1},... | collective-permute-start | bytes 196616 | tf_op jit(solution)/shard_map/ppermute | solution.py:60
  38.2 15.3 %collective-permute-start.1 = (f32[512,64]{1,0:T(8,128)S(1)}, f32[512,64]{1,0:T(8,128)S(1)}, u32[]{:S(2)}, u32[]{:S(2)}) collective-permute-start(f32[512,64]{1,0:T(8,128)S(1)} %squeeze.44), channel_id=1, source_target_pairs={{30,0},{31,1},{0,2},{1,3},{2,4},{3,5},{4,6},{5,7},{6,8},{7,9},{8,1... | collective-permute-start | bytes 393224 | tf_op jit(solution)/shard_map/ppermute | solution.py:13
  39.1 14.4 %collective-permute-start.2 = (f32[512,64]{1,0:T(8,128)S(1)}, f32[512,64]{1,0:T(8,128)S(1)}, u32[]{:S(2)}, u32[]{:S(2)}) collective-permute-start(f32[512,64]{1,0:T(8,128)S(1)} %squeeze.45), channel_id=1, source_target_pairs={{29,0},{30,1},{31,2},{0,3},{1,4},{2,5},{3,6},{4,7},{5,8},{6,9},{7,... | collective-permute-start | bytes 393224 | tf_op jit(solution)/shard_map/ppermute | solution.py:13
  40.0 13.5 %collective-permute-start.3 = (f32[512,64]{1,0:T(8,128)}, f32[512,64]{1,0:T(8,128)S(1)}, u32[]{:S(2)}, u32[]{:S(2)}) collective-permute-start(f32[512,64]{1,0:T(8,128)} %squeeze.46), channel_id=1, source_target_pairs={{1,0},{2,1},{3,2},{4,3},{5,4},{6,5},{7,6},{8,7},{9,8},{10,9},{11,1... | collective-permute-start | bytes 393224 | tf_op jit(solution)/shard_map/ppermute | solution.py:13
  47.1 12.7 %collective-permute-start.4 = (f32[512,64]{1,0:T(8,128)}, f32[512,64]{1,0:T(8,128)S(1)}, u32[]{:S(2)}, u32[]{:S(2)}) collective-permute-start(f32[512,64]{1,0:T(8,128)} %squeeze.47), channel_id=1, source_target_pairs={{2,0},{3,1},{4,2},{5,3},{6,4},{7,5},{8,6},{9,7},{10,8},{11,9},{12,... | collective-permute-start | bytes 393224 | tf_op jit(solution)/shard_map/ppermute | solution.py:13
  47.7 17.0 %collective-permute-start.5 = (f32[512,64]{1,0:T(8,128)}, f32[512,64]{1,0:T(8,128)S(1)}, u32[]{:S(2)}, u32[]{:S(2)}) collective-permute-start(f32[512,64]{1,0:T(8,128)} %squeeze.48), channel_id=1, source_target_pairs={{3,0},{4,1},{5,2},{6,3},{7,4},{8,5},{9,6},{10,7},{11,8},{12,9},{13... | collective-permute-start | bytes 393224 | tf_op jit(solution)/shard_map/ppermute | solution.py:13
  53.5 16.7 %collective-permute-start.10 = (f32[256,64]{1,0:T(8,128)S(1)}, f32[256,64]{1,0:T(8,128)S(1)}, u32[]{:S(2)}, u32[]{:S(2)}) collective-permute-start(f32[256,64]{1,0:T(8,128)S(1)} %add.94), channel_id=1, source_target_pairs={{0,16},{1,17},{2,18},{3,19},{4,20},{5,21},{6,22},{7,23},{8,24},{9,... | collective-permute-start | bytes 196616 | tf_op jit(solution)/shard_map/ppermute | solution.py:60
  84.0 29.8 %copy-start.2 = (bf16[256,64]{0,1:T(8,128)(2,1)S(1)}, bf16[256,64]{0,1:T(8,128)(2,1)}, u32[]{:S(2)}) copy-start(bf16[256,64]{0,1:T(8,128)(2,1)} %param.8) | copy-start | bytes 98308
  88.5 25.4 %copy-start = (bf16[512,64]{0,1:T(8,128)(2,1)S(1)}, bf16[512,64]{0,1:T(8,128)(2,1)}, u32[]{:S(2)}) copy-start(bf16[512,64]{0,1:T(8,128)(2,1)} %param.7) | copy-start | bytes 196612
  88.7 1.4 %collective-permute-start.17 = (f32[256,64]{1,0:T(8,128)S(1)}, f32[256,64]{1,0:T(8,128)S(1)}, u32[]{:S(2)}, u32[]{:S(2)}) collective-permute-start(f32[256,64]{1,0:T(8,128)S(1)} %reshape.63), channel_id=1, source_target_pairs={{0,1},{1,0},{2,3},{3,2},{4,5},{5,4},{6,7},{7,6},{8,9},{9,8},{10,11... | collective-permute-start | bytes 196616 | tf_op jit(solution)/shard_map/ppermute | solution.py:60
  90.1 6.4 %collective-permute-start.18 = (f32[256,64]{1,0:T(8,128)S(1)}, f32[256,64]{1,0:T(8,128)S(1)}, u32[]{:S(2)}, u32[]{:S(2)}) collective-permute-start(f32[256,64]{1,0:T(8,128)S(1)} %add.104), channel_id=1, source_target_pairs={{0,2},{1,3},{2,0},{3,1},{4,6},{5,7},{6,4},{7,5},{8,10},{9,11},{10,... | collective-permute-start | bytes 196616 | tf_op jit(solution)/shard_map/ppermute | solution.py:60
  90.6 22.7 %collective-permute-start.11 = (f32[512,64]{1,0:T(8,128)S(1)}, f32[512,64]{1,0:T(8,128)S(1)}, u32[]{:S(2)}, u32[]{:S(2)}) collective-permute-start(f32[512,64]{1,0:T(8,128)S(1)} %squeeze.50), channel_id=1, source_target_pairs={{31,0},{0,1},{1,2},{2,3},{3,4},{4,5},{5,6},{6,7},{7,8},{8,9},{9,10... | collective-permute-start | bytes 393224 | tf_op jit(solution)/shard_map/ppermute | solution.py:13
  96.6 6.2 %collective-permute-start.19 = (f32[256,64]{1,0:T(8,128)S(1)}, f32[256,64]{1,0:T(8,128)S(1)}, u32[]{:S(2)}, u32[]{:S(2)}) collective-permute-start(f32[256,64]{1,0:T(8,128)S(1)} %add.105), channel_id=1, source_target_pairs={{0,4},{1,5},{2,6},{3,7},{4,0},{5,1},{6,2},{7,3},{8,12},{9,13},{10,... | collective-permute-start | bytes 196616 | tf_op jit(solution)/shard_map/ppermute | solution.py:60
  102.8 10.5 %collective-permute-start.20 = (f32[256,64]{1,0:T(8,128)S(1)}, f32[256,64]{1,0:T(8,128)S(1)}, u32[]{:S(2)}, u32[]{:S(2)}) collective-permute-start(f32[256,64]{1,0:T(8,128)S(1)} %add.106), channel_id=1, source_target_pairs={{0,8},{1,9},{2,10},{3,11},{4,12},{5,13},{6,14},{7,15},{8,0},{9,1},... | collective-permute-start | bytes 196616 | tf_op jit(solution)/shard_map/ppermute | solution.py:60
  103.8 15.5 %collective-permute-start.12 = (f32[512,64]{1,0:T(8,128)}, f32[512,64]{1,0:T(8,128)S(1)}, u32[]{:S(2)}, u32[]{:S(2)}) collective-permute-start(f32[512,64]{1,0:T(8,128)} %squeeze.51), channel_id=1, source_target_pairs={{30,0},{31,1},{0,2},{1,3},{2,4},{3,5},{4,6},{5,7},{6,8},{7,9},{8,1... | collective-permute-start | bytes 393224 | tf_op jit(solution)/shard_map/ppermute | solution.py:13
  104.0 15.3 %collective-permute-start.13 = (f32[512,64]{1,0:T(8,128)S(1)}, f32[512,64]{1,0:T(8,128)S(1)}, u32[]{:S(2)}, u32[]{:S(2)}) collective-permute-start(f32[512,64]{1,0:T(8,128)S(1)} %squeeze.52), channel_id=1, source_target_pairs={{29,0},{30,1},{31,2},{0,3},{1,4},{2,5},{3,6},{4,7},{5,8},{6,9},{7,... | collective-permute-start | bytes 393224 | tf_op jit(solution)/shard_map/ppermute | solution.py:13
  105.6 13.6 %collective-permute-start.14 = (f32[512,64]{1,0:T(8,128)}, f32[512,64]{1,0:T(8,128)S(1)}, u32[]{:S(2)}, u32[]{:S(2)}) collective-permute-start(f32[512,64]{1,0:T(8,128)} %squeeze.53), channel_id=1, source_target_pairs={{1,0},{2,1},{3,2},{4,3},{5,4},{6,5},{7,6},{8,7},{9,8},{10,9},{11,1... | collective-permute-start | bytes 393224 | tf_op jit(solution)/shard_map/ppermute | solution.py:13
  113.3 12.4 %collective-permute-start.15 = (f32[512,64]{1,0:T(8,128)}, f32[512,64]{1,0:T(8,128)S(1)}, u32[]{:S(2)}, u32[]{:S(2)}) collective-permute-start(f32[512,64]{1,0:T(8,128)} %squeeze.54), channel_id=1, source_target_pairs={{2,0},{3,1},{4,2},{5,3},{6,4},{7,5},{8,6},{9,7},{10,8},{11,9},{12,... | collective-permute-start | bytes 393224 | tf_op jit(solution)/shard_map/ppermute | solution.py:13
  113.3 0.8 copy-start.1
  113.3 17.6 %collective-permute-start.16 = (f32[512,64]{1,0:T(8,128)}, f32[512,64]{1,0:T(8,128)S(1)}, u32[]{:S(2)}, u32[]{:S(2)}) collective-permute-start(f32[512,64]{1,0:T(8,128)} %squeeze.55), channel_id=1, source_target_pairs={{3,0},{4,1},{5,2},{6,3},{7,4},{8,5},{9,6},{10,7},{11,8},{12,9},{13... | collective-permute-start | bytes 393224 | tf_op jit(solution)/shard_map/ppermute | solution.py:13
  119.2 16.9 %collective-permute-start.21 = (f32[256,64]{1,0:T(8,128)S(1)}, f32[256,64]{1,0:T(8,128)S(1)}, u32[]{:S(2)}, u32[]{:S(2)}) collective-permute-start(f32[256,64]{1,0:T(8,128)S(1)} %add.107), channel_id=1, source_target_pairs={{0,16},{1,17},{2,18},{3,19},{4,20},{5,21},{6,22},{7,23},{8,24},{9,... | collective-permute-start | bytes 196616 | tf_op jit(solution)/shard_map/ppermute | solution.py:60
